TPU v7x, 8 devices: a whole 2x2x1 slice. The times are simulated.
8 devices in a mesh: dp: 1 (over z), tp: 8 (over y, x, core).
Axes of the slice: x: 2, y: 2, z: 1, core: 2. Of those that a mesh axis runs over, the one named last changes fastest.
Arguments:
- x_in: bfloat16 [1536, 2048], P('dp')
- g_norm: bfloat16 [2048], replicated
- w_q: bfloat16 [2048, 2048], P(None, 'tp')
- w_k: bfloat16 [2048, 1024], replicated
- w_v: bfloat16 [2048, 1024], replicated
- w_o: bfloat16 [2048, 2048], P('tp')
- w_gate: bfloat16 [2048, 6144], P(None, 'tp')
- w_up: bfloat16 [2048, 6144], P(None, 'tp')
- w_down: bfloat16 [6144, 2048], P('tp')
Outputs:
- output 1: bfloat16 [1536, 2048], P('dp')
- output 2: bfloat16 [1536, 8, 128], P('dp', 'tp')
- output 3: bfloat16 [1536, 8, 128], P('dp', 'tp')
All inputs are finite; a program needn't handle non-finite values.
Results may differ from a plain program's by a relative error of at most 0.0113708.
Values are sent between devices in bfloat16 or wider.
A program may use at most 1 GiB of HBM per device.

v0:
```python
import math
import jax
import jax.numpy as jnp
from jax import lax
from jax.sharding import PartitionSpec as P

HEAD_DIM = 128
ROPE_BASE = 500000.0
NORM_EPS = 1e-5


def rope_tables(positions):
    inv_freq = ROPE_BASE ** (-jnp.arange(0, HEAD_DIM, 2, dtype=jnp.float32) / HEAD_DIM)
    angles = positions.astype(jnp.float32)[:, None] * inv_freq[None, :]
    return jnp.cos(angles), jnp.sin(angles)


def apply_rope(projected, cos_tab, sin_tab):
    half_dim = HEAD_DIM // 2
    lower_half = projected[..., :half_dim]
    upper_half = projected[..., half_dim:]
    cos_b = cos_tab[:, None, :]
    sin_b = sin_tab[:, None, :]
    return jnp.concatenate([lower_half * cos_b - upper_half * sin_b, upper_half * cos_b + lower_half * sin_b], axis=-1)


def rms_norm(x_rows, g_norm):
    x_f32 = x_rows.astype(jnp.float32)
    inv_rms = lax.rsqrt(jnp.mean(x_f32 * x_f32, axis=-1, keepdims=True) + NORM_EPS)
    return (x_f32 * inv_rms * g_norm.astype(jnp.float32)).astype(jnp.bfloat16)


def solution(mesh):
    tp_size = mesh.shape['tp']

    def local_layer(x_in, g_norm, w_q, w_k, w_v, w_o, w_gate, w_up, w_down):
        tokens, width = x_in.shape
        kv_heads = w_k.shape[1] // HEAD_DIM
        kv_local = max(kv_heads // tp_size, 1)
        q_local = w_q.shape[1] // HEAD_DIM
        group_size = q_local // kv_local
        q_block = min(128, tokens)
        score_scale = 1.0 / math.sqrt(HEAD_DIM)
        head_start = lax.axis_index('tp') * kv_heads // tp_size
        normed = rms_norm(x_in, g_norm)
        cos_tab, sin_tab = rope_tables(jnp.arange(tokens))
        w_k_mine = lax.dynamic_slice_in_dim(w_k, head_start * HEAD_DIM, kv_local * HEAD_DIM, axis=1)
        w_v_mine = lax.dynamic_slice_in_dim(w_v, head_start * HEAD_DIM, kv_local * HEAD_DIM, axis=1)
        k_proj = jnp.dot(normed, w_k_mine, preferred_element_type=jnp.float32).reshape(tokens, kv_local, HEAD_DIM)
        k_rot = apply_rope(k_proj, cos_tab, sin_tab).astype(jnp.bfloat16)
        v_proj = jnp.dot(normed, w_v_mine, preferred_element_type=jnp.float32).astype(jnp.bfloat16).reshape(tokens, kv_local, HEAD_DIM)
        key_pos = jnp.arange(tokens)

        def row_block(block_idx):
            row_start = block_idx * q_block
            normed_blk = lax.dynamic_slice_in_dim(normed, row_start, q_block, axis=0)
            cos_blk = lax.dynamic_slice_in_dim(cos_tab, row_start, q_block, axis=0)
            sin_blk = lax.dynamic_slice_in_dim(sin_tab, row_start, q_block, axis=0)
            q_proj = jnp.dot(normed_blk, w_q, preferred_element_type=jnp.float32).reshape(q_block, q_local, HEAD_DIM)
            q_rot = apply_rope(q_proj, cos_blk, sin_blk).astype(jnp.bfloat16).reshape(q_block, kv_local, group_size, HEAD_DIM)
            scores = jnp.einsum('qgrd,kgd->grqk', q_rot, k_rot, preferred_element_type=jnp.float32) * score_scale
            query_pos = row_start + jnp.arange(q_block)
            scores = jnp.where(key_pos[None, :] <= query_pos[:, None], scores, -1e30)
            probs_bf = jax.nn.softmax(scores, axis=-1).astype(jnp.bfloat16)
            attn_out = jnp.einsum('grqk,kgd->qgrd', probs_bf, v_proj, preferred_element_type=jnp.float32).astype(jnp.bfloat16).reshape(q_block, q_local * HEAD_DIM)
            gate_proj = jnp.dot(normed_blk, w_gate, preferred_element_type=jnp.float32)
            up_proj = jnp.dot(normed_blk, w_up, preferred_element_type=jnp.float32)
            hidden = (jax.nn.silu(gate_proj) * up_proj).astype(jnp.bfloat16)
            return (jnp.dot(attn_out, w_o, preferred_element_type=jnp.float32) + jnp.dot(hidden, w_down, preferred_element_type=jnp.float32)).astype(jnp.bfloat16)

        partial_sum = lax.map(row_block, jnp.arange(tokens // q_block)).reshape(tokens, width)
        reduced_sum = lax.psum(partial_sum, 'tp')
        y_out = (x_in.astype(jnp.float32) + reduced_sum.astype(jnp.float32)).astype(jnp.bfloat16)
        return y_out, k_rot, v_proj

    return jax.shard_map(local_layer, mesh=mesh, in_specs=(P('dp', None), P(None), P(None, 'tp'), P(None, None), P(None, None), P('tp', None), P(None, 'tp'), P(None, 'tp'), P('tp', None)), out_specs=(P('dp', None), P('dp', 'tp', None), P('dp', 'tp', None)), check_vma=False)
```

profile of v0, /device:TPU:0, one launch (start us, length us, event | category | flops | bytes accessed | tf_op | source)
XLA Modules:
  0.0 322.8 jit_solution(17135590261942933495)
XLA Ops:
  7.3 4.1 %fusion.33 = f32[1536]{0:T(1024)S(1)} fusion(bf16[1536,2048]{1,0:T(8,128)(2,1)} %param.11), kind=kLoop, calls=%fused_computation.45 | loop fusion | flops 9435648 | bytes 6297600 | tf_op jit(solution)/shard_map/reduce_sum | solution.py:29
  11.4 4.3 %fusion.35 = bf16[1536,2048]{1,0:T(8,128)(2,1)S(1)} fusion(bf16[1536,2048]{1,0:T(8,128)(2,1)} %param.11, f32[2048]{0:T(1024)S(1)} %convert_element_type.70, f32[1536]{0:T(1024)S(1)} %add_rsqrt_fusion), kind=kLoop, calls=%fused_computation.47 | loop fusion | flops 12582912 | bytes 12597248 | tf_op jit(solution)/shard_map/convert_element_type | solution.py:30
  15.7 5.0 %multiply_sine_fusion = (f32[1536,64]{1,0:T(8,128)}, f32[1536,64]{1,0:T(8,128)}) fusion(f32[64]{0:T(128)S(1)} %multiply_power_fusion, f32[1536]{0:T(1024)S(1)} %iota_convert_fusion), kind=kLoop, calls=%fused_computation.52 | loop fusion | flops 98304 | bytes 792832 | tf_op jit(solution)/shard_map/sin | solution.py:15
  20.7 3.3 %convolution_bitcast_fusion = f32[1536,1,128]{0,2,1:T(8,128)S(1)} fusion(bf16[1536,2048]{1,0:T(8,128)(2,1)S(1)} %fusion.35, bf16[2048,1024]{1,0:T(8,128)(2,1)} %param.14, s32[]{:T(128)S(6)} %select_n.19), kind=kOutput, calls=%fused_computation.49 | convolution fusion | flops 805306368 | bytes 7602180 | tf_op jit(solution)/shard_map/dot_general | solution.py:49
  24.0 1.6 fusion.45
  26.6 4.7 %fusion.37 = bf16[1536,1,128]{2,0,1:T(8,128)(2,1)S(1)} fusion(bf16[1536,2048]{1,0:T(8,128)(2,1)} %copy-done, bf16[2048,1024]{1,0:T(8,128)(2,1)} %param.15, s32[]{:T(128)S(6)} %select_n.19), kind=kOutput, calls=%fused_computation.51 | convolution fusion | flops 805502976 | bytes 7208964 | tf_op jit(solution)/shard_map/dot_general | solution.py:51
  32.3 177.3 %while.11 = (s32[]{:T(128)}, bf16[12,128,2048]{2,1,0:T(8,128)(2,1)}, s32[12]{0:T(128)S(1)}, bf16[1536,2048]{1,0:T(8,128)(2,1)}, bf16[2048,256]{1,0:T(8,128)(2,1)...) while((s32[]{:T(128)}, ...), condition=%wide.region_4.5_spmd.clone, body=%wide.region_1.4_spmd.clone.sunk | while | flops 1682472576 | bytes 36248328 | solution.py:71
  33.6 1.4 fusion.90
  36.4 1.7 fusion.92
  38.5 1.5 convolution_convert_fusion.3
  40.3 1.6 fusion.95
  42.0 5.1 %fusion.96 = bf16[12,128,2048]{2,1,0:T(8,128)(2,1)} fusion(bf16[12,128,2048]{2,1,0:T(8,128)(2,1)} %get-tuple-element.271, s32[]{:T(128)} %get-tuple-element.270, f32[128,2048]{1,0:T(8,128)S(1)} %fusion.94, bf16[768,2048]{1,0:T(8,128)(2,1)} %get-tuple-element.299, bf16[2048,768]{1,0:T(8,128)(2,1)} %get-tuple-element.298, ...), kind=kOutput, calls=%fused_computation.7.clone.1 | convolution fusion | flops 806420480 | bytes 8782340 | tf_op jit(solution)/shard_map/while/body/eval_jaxpr/dot_general | solution.py:69
  48.4 1.4 fusion.90
  51.2 1.7 fusion.92
  53.3 1.5 convolution_convert_fusion.3
  55.1 1.6 fusion.95
  56.7 5.1 %fusion.96 = bf16[12,128,2048]{2,1,0:T(8,128)(2,1)} fusion(bf16[12,128,2048]{2,1,0:T(8,128)(2,1)} %get-tuple-element.271, s32[]{:T(128)} %get-tuple-element.270, f32[128,2048]{1,0:T(8,128)S(1)} %fusion.94, bf16[768,2048]{1,0:T(8,128)(2,1)} %get-tuple-element.299, bf16[2048,768]{1,0:T(8,128)(2,1)} %get-tuple-element.298, ...), kind=kOutput, calls=%fused_computation.7.clone.1 | convolution fusion | flops 806420480 | bytes 8782340 | tf_op jit(solution)/shard_map/while/body/eval_jaxpr/dot_general | solution.py:69
  63.2 1.4 fusion.90
  65.9 1.7 fusion.92
  68.0 1.5 convolution_convert_fusion.3
  69.9 1.6 fusion.95
  71.5 5.1 %fusion.96 = bf16[12,128,2048]{2,1,0:T(8,128)(2,1)} fusion(bf16[12,128,2048]{2,1,0:T(8,128)(2,1)} %get-tuple-element.271, s32[]{:T(128)} %get-tuple-element.270, f32[128,2048]{1,0:T(8,128)S(1)} %fusion.94, bf16[768,2048]{1,0:T(8,128)(2,1)} %get-tuple-element.299, bf16[2048,768]{1,0:T(8,128)(2,1)} %get-tuple-element.298, ...), kind=kOutput, calls=%fused_computation.7.clone.1 | convolution fusion | flops 806420480 | bytes 8782340 | tf_op jit(solution)/shard_map/while/body/eval_jaxpr/dot_general | solution.py:69
  80.7 1.7 fusion.92
  82.8 1.5 convolution_convert_fusion.3
  84.7 1.6 fusion.95
  86.3 5.1 %fusion.96 = bf16[12,128,2048]{2,1,0:T(8,128)(2,1)} fusion(bf16[12,128,2048]{2,1,0:T(8,128)(2,1)} %get-tuple-element.271, s32[]{:T(128)} %get-tuple-element.270, f32[128,2048]{1,0:T(8,128)S(1)} %fusion.94, bf16[768,2048]{1,0:T(8,128)(2,1)} %get-tuple-element.299, bf16[2048,768]{1,0:T(8,128)(2,1)} %get-tuple-element.298, ...), kind=kOutput, calls=%fused_computation.7.clone.1 | convolution fusion | flops 806420480 | bytes 8782340 | tf_op jit(solution)/shard_map/while/body/eval_jaxpr/dot_general | solution.py:69
  92.7 1.4 fusion.90
  95.5 1.7 fusion.92
  97.6 1.5 convolution_convert_fusion.3
  99.4 1.6 fusion.95
  101.1 5.1 %fusion.96 = bf16[12,128,2048]{2,1,0:T(8,128)(2,1)} fusion(bf16[12,128,2048]{2,1,0:T(8,128)(2,1)} %get-tuple-element.271, s32[]{:T(128)} %get-tuple-element.270, f32[128,2048]{1,0:T(8,128)S(1)} %fusion.94, bf16[768,2048]{1,0:T(8,128)(2,1)} %get-tuple-element.299, bf16[2048,768]{1,0:T(8,128)(2,1)} %get-tuple-element.298, ...), kind=kOutput, calls=%fused_computation.7.clone.1 | convolution fusion | flops 806420480 | bytes 8782340 | tf_op jit(solution)/shard_map/while/body/eval_jaxpr/dot_general | solution.py:69
  107.5 1.4 fusion.90
  110.3 1.7 fusion.92
  112.3 1.5 convolution_convert_fusion.3
  114.2 1.6 fusion.95
  115.8 5.1 %fusion.96 = bf16[12,128,2048]{2,1,0:T(8,128)(2,1)} fusion(bf16[12,128,2048]{2,1,0:T(8,128)(2,1)} %get-tuple-element.271, s32[]{:T(128)} %get-tuple-element.270, f32[128,2048]{1,0:T(8,128)S(1)} %fusion.94, bf16[768,2048]{1,0:T(8,128)(2,1)} %get-tuple-element.299, bf16[2048,768]{1,0:T(8,128)(2,1)} %get-tuple-element.298, ...), kind=kOutput, calls=%fused_computation.7.clone.1 | convolution fusion | flops 806420480 | bytes 8782340 | tf_op jit(solution)/shard_map/while/body/eval_jaxpr/dot_general | solution.py:69
  125.0 1.7 fusion.92
  127.1 1.5 convolution_convert_fusion.3
  129.0 1.6 fusion.95
  130.6 5.1 %fusion.96 = bf16[12,128,2048]{2,1,0:T(8,128)(2,1)} fusion(bf16[12,128,2048]{2,1,0:T(8,128)(2,1)} %get-tuple-element.271, s32[]{:T(128)} %get-tuple-element.270, f32[128,2048]{1,0:T(8,128)S(1)} %fusion.94, bf16[768,2048]{1,0:T(8,128)(2,1)} %get-tuple-element.299, bf16[2048,768]{1,0:T(8,128)(2,1)} %get-tuple-element.298, ...), kind=kOutput, calls=%fused_computation.7.clone.1 | convolution fusion | flops 806420480 | bytes 8782340 | tf_op jit(solution)/shard_map/while/body/eval_jaxpr/dot_general | solution.py:69
  137.0 1.4 fusion.90
  139.8 1.7 fusion.92
  141.9 1.5 convolution_convert_fusion.3
  143.7 1.6 fusion.95
  145.4 5.1 %fusion.96 = bf16[12,128,2048]{2,1,0:T(8,128)(2,1)} fusion(bf16[12,128,2048]{2,1,0:T(8,128)(2,1)} %get-tuple-element.271, s32[]{:T(128)} %get-tuple-element.270, f32[128,2048]{1,0:T(8,128)S(1)} %fusion.94, bf16[768,2048]{1,0:T(8,128)(2,1)} %get-tuple-element.299, bf16[2048,768]{1,0:T(8,128)(2,1)} %get-tuple-element.298, ...), kind=kOutput, calls=%fused_computation.7.clone.1 | convolution fusion | flops 806420480 | bytes 8782340 | tf_op jit(solution)/shard_map/while/body/eval_jaxpr/dot_general | solution.py:69
  151.8 1.4 fusion.90
  154.6 1.7 fusion.92
  156.7 1.5 convolution_convert_fusion.3
  158.5 1.6 fusion.95
  160.1 5.1 %fusion.96 = bf16[12,128,2048]{2,1,0:T(8,128)(2,1)} fusion(bf16[12,128,2048]{2,1,0:T(8,128)(2,1)} %get-tuple-element.271, s32[]{:T(128)} %get-tuple-element.270, f32[128,2048]{1,0:T(8,128)S(1)} %fusion.94, bf16[768,2048]{1,0:T(8,128)(2,1)} %get-tuple-element.299, bf16[2048,768]{1,0:T(8,128)(2,1)} %get-tuple-element.298, ...), kind=kOutput, calls=%fused_computation.7.clone.1 | convolution fusion | flops 806420480 | bytes 8782340 | tf_op jit(solution)/shard_map/while/body/eval_jaxpr/dot_general | solution.py:69
  169.3 1.7 fusion.92
  171.4 1.5 convolution_convert_fusion.3
  173.3 1.6 fusion.95
  174.9 5.1 %fusion.96 = bf16[12,128,2048]{2,1,0:T(8,128)(2,1)} fusion(bf16[12,128,2048]{2,1,0:T(8,128)(2,1)} %get-tuple-element.271, s32[]{:T(128)} %get-tuple-element.270, f32[128,2048]{1,0:T(8,128)S(1)} %fusion.94, bf16[768,2048]{1,0:T(8,128)(2,1)} %get-tuple-element.299, bf16[2048,768]{1,0:T(8,128)(2,1)} %get-tuple-element.298, ...), kind=kOutput, calls=%fused_computation.7.clone.1 | convolution fusion | flops 806420480 | bytes 8782340 | tf_op jit(solution)/shard_map/while/body/eval_jaxpr/dot_general | solution.py:69
  184.1 1.7 fusion.92
  186.2 1.5 convolution_convert_fusion.3
  188.1 1.6 fusion.95
  189.7 5.1 %fusion.96 = bf16[12,128,2048]{2,1,0:T(8,128)(2,1)} fusion(bf16[12,128,2048]{2,1,0:T(8,128)(2,1)} %get-tuple-element.271, s32[]{:T(128)} %get-tuple-element.270, f32[128,2048]{1,0:T(8,128)S(1)} %fusion.94, bf16[768,2048]{1,0:T(8,128)(2,1)} %get-tuple-element.299, bf16[2048,768]{1,0:T(8,128)(2,1)} %get-tuple-element.298, ...), kind=kOutput, calls=%fused_computation.7.clone.1 | convolution fusion | flops 806420480 | bytes 8782340 | tf_op jit(solution)/shard_map/while/body/eval_jaxpr/dot_general | solution.py:69
  198.9 1.7 fusion.92
  201.0 1.5 convolution_convert_fusion.3
  202.8 1.6 fusion.95
  204.5 5.1 %fusion.96 = bf16[12,128,2048]{2,1,0:T(8,128)(2,1)} fusion(bf16[12,128,2048]{2,1,0:T(8,128)(2,1)} %get-tuple-element.271, s32[]{:T(128)} %get-tuple-element.270, f32[128,2048]{1,0:T(8,128)S(1)} %fusion.94, bf16[768,2048]{1,0:T(8,128)(2,1)} %get-tuple-element.299, bf16[2048,768]{1,0:T(8,128)(2,1)} %get-tuple-element.298, ...), kind=kOutput, calls=%fused_computation.7.clone.1 | convolution fusion | flops 806420480 | bytes 8782340 | tf_op jit(solution)/shard_map/while/body/eval_jaxpr/dot_general | solution.py:69
  209.6 95.3 %all-reduce.2.cloned.1.call-done = bf16[1536,2048]{1,0:T(8,128)(2,1)} async-done(((bf16[1536,2048]{1,0:T(8,128)(2,1)}), bf16[1536,2048]{1,0:T(8,128)(2,1)}) %all-reduce.2.cloned.1.call-update) | async-done | bytes 6291472 | tf_op jit(solution)/shard_map/psum | solution.py:72
  304.9 11.0 %fusion.36 = bf16[1536,2048]{1,0:T(8,128)(2,1)} fusion(bf16[1536,2048]{1,0:T(8,128)(2,1)} %param.11, bf16[1536,2048]{1,0:T(8,128)(2,1)} %all-reduce.2.cloned.1.call-done), kind=kLoop, calls=%fused_computation.48 | loop fusion | flops 12582912 | bytes 18874368 | tf_op jit(solution)/shard_map/convert_element_type | solution.py:73
  (158 shorter events, 41.6 us)
Async XLA Ops:
  7.2 4.2 %copy-start.5 = (bf16[2048]{0:T(1024)(128)(2,1)S(1)}, bf16[2048]{0:T(1024)(128)(2,1)}, u32[]{:S(2)}) copy-start(bf16[2048]{0:T(1024)(128)(2,1)} %param.12) | copy-start | bytes 12292
  7.2 297.7 %all-reduce.2.cloned.1.call-start = ((), (), s32[]{:S(2)}) async-start(), calls=%async_computation | async-start | bytes 12582912 | tf_op jit(solution)/shard_map/psum | solution.py:72
  15.7 10.0 %copy-start = (bf16[1536,2048]{1,0:T(8,128)(2,1)}, bf16[1536,2048]{1,0:T(8,128)(2,1)S(1)}, u32[]{:S(2)}) copy-start(bf16[1536,2048]{1,0:T(8,128)(2,1)S(1)} %fusion.35) | copy-start | bytes 18874372
  24.0 8.3 %copy-start.2 = (bf16[2048,256]{1,0:T(8,128)(2,1)S(1)}, bf16[2048,256]{1,0:T(8,128)(2,1)}, u32[]{:S(2)}) copy-start(bf16[2048,256]{1,0:T(8,128)(2,1)} %param.13) | copy-start | bytes 3145732
  24.0 8.2 %copy-start.3 = (bf16[256,2048]{1,0:T(8,128)(2,1)S(1)}, bf16[256,2048]{1,0:T(8,128)(2,1)}, u32[]{:S(2)}) copy-start(bf16[256,2048]{1,0:T(8,128)(2,1)} %param.16) | copy-start | bytes 3145732
  31.3 1.0 copy-start.4
  36.4 3.9 %copy-start.1 = (bf16[2048,768]{1,0:T(8,128)(2,1)S(1)}, bf16[2048,768]{1,0:T(8,128)(2,1)}, u32[]{:S(2)}) copy-start(bf16[2048,768]{1,0:T(8,128)(2,1)} %get-tuple-element.297) | copy-start | bytes 9437188 | tf_op jit(solution)/shard_map/while
  51.2 3.9 %copy-start.1 = (bf16[2048,768]{1,0:T(8,128)(2,1)S(1)}, bf16[2048,768]{1,0:T(8,128)(2,1)}, u32[]{:S(2)}) copy-start(bf16[2048,768]{1,0:T(8,128)(2,1)} %get-tuple-element.297) | copy-start | bytes 9437188 | tf_op jit(solution)/shard_map/while
  65.9 3.9 %copy-start.1 = (bf16[2048,768]{1,0:T(8,128)(2,1)S(1)}, bf16[2048,768]{1,0:T(8,128)(2,1)}, u32[]{:S(2)}) copy-start(bf16[2048,768]{1,0:T(8,128)(2,1)} %get-tuple-element.297) | copy-start | bytes 9437188 | tf_op jit(solution)/shard_map/while
  80.7 3.9 %copy-start.1 = (bf16[2048,768]{1,0:T(8,128)(2,1)S(1)}, bf16[2048,768]{1,0:T(8,128)(2,1)}, u32[]{:S(2)}) copy-start(bf16[2048,768]{1,0:T(8,128)(2,1)} %get-tuple-element.297) | copy-start | bytes 9437188 | tf_op jit(solution)/shard_map/while
  95.5 3.9 %copy-start.1 = (bf16[2048,768]{1,0:T(8,128)(2,1)S(1)}, bf16[2048,768]{1,0:T(8,128)(2,1)}, u32[]{:S(2)}) copy-start(bf16[2048,768]{1,0:T(8,128)(2,1)} %get-tuple-element.297) | copy-start | bytes 9437188 | tf_op jit(solution)/shard_map/while
  110.2 3.9 %copy-start.1 = (bf16[2048,768]{1,0:T(8,128)(2,1)S(1)}, bf16[2048,768]{1,0:T(8,128)(2,1)}, u32[]{:S(2)}) copy-start(bf16[2048,768]{1,0:T(8,128)(2,1)} %get-tuple-element.297) | copy-start | bytes 9437188 | tf_op jit(solution)/shard_map/while
  125.0 3.9 %copy-start.1 = (bf16[2048,768]{1,0:T(8,128)(2,1)S(1)}, bf16[2048,768]{1,0:T(8,128)(2,1)}, u32[]{:S(2)}) copy-start(bf16[2048,768]{1,0:T(8,128)(2,1)} %get-tuple-element.297) | copy-start | bytes 9437188 | tf_op jit(solution)/shard_map/while
  139.8 3.9 %copy-start.1 = (bf16[2048,768]{1,0:T(8,128)(2,1)S(1)}, bf16[2048,768]{1,0:T(8,128)(2,1)}, u32[]{:S(2)}) copy-start(bf16[2048,768]{1,0:T(8,128)(2,1)} %get-tuple-element.297) | copy-start | bytes 9437188 | tf_op jit(solution)/shard_map/while
  154.6 3.9 %copy-start.1 = (bf16[2048,768]{1,0:T(8,128)(2,1)S(1)}, bf16[2048,768]{1,0:T(8,128)(2,1)}, u32[]{:S(2)}) copy-start(bf16[2048,768]{1,0:T(8,128)(2,1)} %get-tuple-element.297) | copy-start | bytes 9437188 | tf_op jit(solution)/shard_map/while
  169.3 3.9 %copy-start.1 = (bf16[2048,768]{1,0:T(8,128)(2,1)S(1)}, bf16[2048,768]{1,0:T(8,128)(2,1)}, u32[]{:S(2)}) copy-start(bf16[2048,768]{1,0:T(8,128)(2,1)} %get-tuple-element.297) | copy-start | bytes 9437188 | tf_op jit(solution)/shard_map/while
  184.1 3.9 %copy-start.1 = (bf16[2048,768]{1,0:T(8,128)(2,1)S(1)}, bf16[2048,768]{1,0:T(8,128)(2,1)}, u32[]{:S(2)}) copy-start(bf16[2048,768]{1,0:T(8,128)(2,1)} %get-tuple-element.297) | copy-start | bytes 9437188 | tf_op jit(solution)/shard_map/while
  198.9 3.9 %copy-start.1 = (bf16[2048,768]{1,0:T(8,128)(2,1)S(1)}, bf16[2048,768]{1,0:T(8,128)(2,1)}, u32[]{:S(2)}) copy-start(bf16[2048,768]{1,0:T(8,128)(2,1)} %get-tuple-element.297) | copy-start | bytes 9437188 | tf_op jit(solution)/shard_map/while
Sparse Core Ops, SparseCore 0:
  209.7 95.1 all-reduce.1
where the time goes:
time: 325 us; the launch traced here: 323 us
  matrix products  147 us (45%)
  waiting for transfers between devices  95.4 us (29%)
  other arithmetic  33.2 us (10%)
  local copies, waits for them, and re-layouts  23.7 us (7%)
  between operations  14.2 us (4%)
  loops' own time  9.18 us (3%)
    psum x1, waiting for transfers between devices, local_layer(): reduced_sum = lax.psum(partial_sum, 'tp')  95.3 us
    dot_general x12, matrix products, row_block(): jnp.dot(hidden, w_down, preferred_element_type=jnp.float32)  60.9 us
    dot_general x12, matrix products, row_block(): jnp.einsum('qgrd,kgd->grqk', q_rot, k_rot, preferred_element_type=jnp.flo...  20.6 us
    dot_general x12, matrix products, row_block(): gate_proj = jnp.dot(normed_blk, w_gate, preferred_element_type=jnp.float32)  19.5 us
    dot_general x12, matrix products, row_block(): jnp.einsum('grqk,kgd->qgrd', probs_bf, v_proj, preferred_element_type=jnp...  18.1 us
    dot_general x12, matrix products, row_block(): jnp.dot(normed_blk, w_q, preferred_element_type=jnp.float32)  16.3 us
    convert_element_type x1, other arithmetic, local_layer(): (x_in.astype(jnp.float32) + reduced_sum.astype(jnp.float32)).astype(jnp.b...  11 us
    dynamic_slice x12, local copies, waits for them, and re-layouts, row_block(): sin_blk = lax.dynamic_slice_in_dim(sin_tab, row_start, q_block, axis=0)  10.6 us
  transfers between devices with their start and end apart: 1, of which 1 were waited for; matrix products, arithmetic and copies ran while one was open for 0% of the time, Pallas kernels for 0%

commit v1 on v0

v1 whole, which is shorter than its diff:
```python
import math
import numpy as np
import jax
import jax.numpy as jnp
from jax import lax
from jax.experimental import pallas as pl
from jax.experimental.pallas import tpu as pltpu
from jax.sharding import PartitionSpec as P

HEAD_DIM = 128
ROPE_BASE = 500000.0
NORM_EPS = 1e-5
TOKENS = 1536
WIDTH = 2048
QCOLS = 256
FFCOLS = 768
ROWS = 256
BLOCKS = TOKENS // ROWS
KDOWN = QCOLS + FFCOLS
LAG_B, LAG_C, LAG_D, LAG_E, LAG_F = 1, 2, 3, 4, 5
SCORE_SCALE = math.log2(math.e) / math.sqrt(HEAD_DIM)
F32 = jnp.float32
BF16 = jnp.bfloat16
MESH = pl.DeviceIdType.MESH

D2D_FIRST, D2D_SECOND, RED_ONE, RED_TWO, GAT_ONE, GAT_TWO, OUT_FIRST, OUT_SECOND = range(8)


def rope_tables():
    inv_freq = np.float32(ROPE_BASE) ** (-np.arange(0, HEAD_DIM, 2, dtype=np.float32) / np.float32(HEAD_DIM))
    angles = np.arange(TOKENS, dtype=np.float32)[:, None] * inv_freq.astype(np.float32)[None, :]
    cos, sin = np.cos(angles.astype(np.float64)), np.sin(angles.astype(np.float64))
    return (np.concatenate([cos, cos], axis=1).astype(np.float32), np.concatenate([-sin, sin], axis=1).astype(np.float32))


def layer_kernel(x_hbm, g_hbm, wq_hbm, wk_hbm, wv_hbm, wo_hbm, wg_hbm, wu_hbm, wd_hbm, cos_hbm, sin_hbm,
                 y_out, k_out, v_out,
                 x_v, g_v, wqkv_v, wg_v, wu_v, wod_v, cos_v, sin_v,
                 a_v, q_v, k_v, v_v, s_v, m_v, l_v, acc_v, om_v,
                 d2d_src, d2d_dst, h_send, h_keep, r1_dst, p_send, p_keep, r2_dst, y_v,
                 x_sem, w_sem, o_sem, kv_sem, ssem, rsem):
    me = lax.axis_index('tp')
    core = lax.rem(me, 2)
    xpos = lax.rem(me // 2, 2)
    ypos = me // 4
    sibling = me + 1 - 2 * core
    xpeer = me + 2 - 4 * xpos
    ypeer = me + 4 - 8 * ypos
    p1 = xpos + core * (ypos - xpos)
    p2 = ypos + core * (xpos - ypos)
    n1 = xpeer + core * (ypeer - xpeer)
    n2 = ypeer + core * (xpeer - ypeer)

    def rows_of(b):
        return pl.ds(pl.multiple_of(b * ROWS, ROWS), ROWS)

    def load_x(b):
        return pltpu.make_async_copy(x_hbm.at[rows_of(b), :], x_v.at[rows_of(b), :], x_sem.at[b])

    kv_cols = pl.ds(pl.multiple_of(me * HEAD_DIM, HEAD_DIM), HEAD_DIM)
    loads = [
        pltpu.make_async_copy(g_hbm, g_v, w_sem.at[0]),
        pltpu.make_async_copy(wk_hbm.at[:, kv_cols], wqkv_v.at[:, pl.ds(QCOLS, HEAD_DIM)], w_sem.at[1]),
        pltpu.make_async_copy(wv_hbm.at[:, kv_cols], wqkv_v.at[:, pl.ds(QCOLS + HEAD_DIM, HEAD_DIM)], w_sem.at[2]),
        pltpu.make_async_copy(wq_hbm, wqkv_v.at[:, pl.ds(0, QCOLS)], w_sem.at[3]),
        pltpu.make_async_copy(cos_hbm, cos_v, w_sem.at[4]),
        pltpu.make_async_copy(sin_hbm, sin_v, w_sem.at[5]),
        pltpu.make_async_copy(wg_hbm, wg_v, w_sem.at[6]),
        pltpu.make_async_copy(wu_hbm, wu_v, w_sem.at[7]),
        pltpu.make_async_copy(wo_hbm, wod_v.at[pl.ds(0, QCOLS), :], w_sem.at[8]),
        pltpu.make_async_copy(wd_hbm, wod_v.at[pl.ds(QCOLS, FFCOLS), :], w_sem.at[9]),
    ]
    load_x(0).start()
    for copy in loads:
        copy.start()
    for b in range(1, BLOCKS):
        load_x(b).start()

    barrier = pltpu.get_barrier_semaphore()
    for peer in (sibling, xpeer, ypeer):
        pl.semaphore_signal(barrier, inc=1, device_id={'tp': peer}, device_id_type=MESH)

    def remote(kind, b, src, dst, peer):
        return pltpu.make_async_remote_copy(src_ref=src, dst_ref=dst, send_sem=ssem.at[kind, b], recv_sem=rsem.at[kind, b],
                                            device_id={'tp': peer}, device_id_type=MESH)

    mine = core * 4 + p1 * 2
    other = core * 4 + (1 - p1) * 2

    def copy_of(kind, b):
        if kind == D2D_FIRST or kind == D2D_SECOND:
            return remote(kind, b, d2d_src.at[b, kind], d2d_dst.at[b, kind], sibling)
        if kind == RED_ONE:
            return remote(kind, b, h_send.at[b], r1_dst.at[b], n1)
        if kind == RED_TWO:
            return remote(kind, b, p_send.at[b], r2_dst.at[b], n2)
        if kind == GAT_ONE:
            piece = mine + p2
            return remote(kind, b, y_v.at[b, piece], y_v.at[b, piece], n2)
        if kind == GAT_TWO:
            return remote(kind, b, y_v.at[b, pl.ds(mine, 2)], y_v.at[b, pl.ds(mine, 2)], n1)
        first = mine if kind == OUT_FIRST else other
        return remote(kind, b, y_v.at[b, pl.ds(first, 2)], y_v.at[b, pl.ds(first, 2)], sibling)

    def store_y(b, piece):
        return pltpu.make_async_copy(y_v.at[b, piece], y_out.at[rows_of(b), pl.ds(pl.multiple_of(piece * 256, 256), 256)],
                                     o_sem.at[b, piece])

    def store_kv(b):
        return (pltpu.make_async_copy(k_v.at[rows_of(b), :], k_out.at[rows_of(b), :], kv_sem.at[0, b]),
                pltpu.make_async_copy(v_v.at[rows_of(b), :], v_out.at[rows_of(b), :], kv_sem.at[1, b]))

    def project(b):
        load_x(b).wait()

        @pl.when(b == 0)
        def _():
            for copy in loads[:1]:
                copy.wait()

        def norm_rows(r, carry):
            sl = pl.ds(pl.multiple_of(b * ROWS + r * 16, 16), 16)
            x_f = x_v[sl, :].astype(F32)
            inv = lax.rsqrt(jnp.mean(x_f * x_f, axis=-1, keepdims=True) + NORM_EPS)
            a_v[pl.ds(pl.multiple_of(r * 16, 16), 16), :] = (x_f * inv * g_v[...].astype(F32)).astype(BF16)
            return carry

        lax.fori_loop(0, ROWS // 16, norm_rows, 0, unroll=4)

        @pl.when(b == 0)
        def _():
            for copy in loads[1:6]:
                copy.wait()

        cos, sin = cos_v[rows_of(b), :], sin_v[rows_of(b), :]
        qkv = jnp.dot(a_v[...], wqkv_v[...], preferred_element_type=F32)

        def rope(h):
            return (h * cos + pltpu.roll(h, HEAD_DIM // 2, 1) * sin).astype(BF16)

        q_v[pl.ds(0, ROWS), :] = rope(qkv[:, 0:128])
        q_v[pl.ds(ROWS, ROWS), :] = rope(qkv[:, 128:256])
        k_v[rows_of(b), :] = rope(qkv[:, 256:384])
        v_v[rows_of(b), :] = qkv[:, 384:512].astype(BF16)
        for copy in store_kv(b):
            copy.start()

    def attend(b):
        def tile(j):
            return pl.ds(pl.multiple_of(j * ROWS, ROWS), ROWS)

        def scores(j):
            s = lax.dot_general(q_v[...], k_v[tile(j), :], (((1,), (1,)), ((), ())), preferred_element_type=F32)
            return s * SCORE_SCALE

        qpos = lax.broadcasted_iota(jnp.int32, (2 * ROWS, ROWS), 0)
        kpos = lax.broadcasted_iota(jnp.int32, (2 * ROWS, ROWS), 1)
        t = jnp.where(kpos <= lax.rem(qpos, ROWS), scores(b), -1e30)
        s_v[:, tile(b)] = t
        m_v[...] = jnp.maximum(t[:, :128], t[:, 128:])

        def score_tile(j, carry):
            t = scores(j)
            s_v[:, tile(j)] = t
            m_v[...] = jnp.maximum(m_v[...], jnp.maximum(t[:, :128], t[:, 128:]))
            return carry

        lax.fori_loop(0, b, score_tile, 0)
        m_v[...] = jnp.broadcast_to(jnp.max(m_v[...], axis=1, keepdims=True), (2 * ROWS, 128))
        l_v[...] = jnp.zeros_like(l_v)

        def exp_tile(j, carry):
            m = m_v[...]
            e0 = jnp.exp2(s_v[:, pl.ds(pl.multiple_of(j * ROWS, ROWS), 128)] - m)
            e1 = jnp.exp2(s_v[:, pl.ds(pl.multiple_of(j * ROWS + 128, 128), 128)] - m)
            s_v[:, pl.ds(pl.multiple_of(j * ROWS, ROWS), 128)] = e0
            s_v[:, pl.ds(pl.multiple_of(j * ROWS + 128, 128), 128)] = e1
            l_v[...] += e0 + e1
            return carry

        lax.fori_loop(0, b + 1, exp_tile, 0)
        l_v[...] = jnp.broadcast_to(1.0 / jnp.sum(l_v[...], axis=1, keepdims=True), (2 * ROWS, 128))
        acc_v[...] = jnp.zeros_like(acc_v)

        def value_tile(j, carry):
            r = l_v[...]
            p = (s_v[:, tile(j)] * jnp.concatenate([r, r], axis=1)).astype(BF16)
            acc_v[...] += jnp.dot(p, v_v[tile(j), :], preferred_element_type=F32)
            return carry

        lax.fori_loop(0, b + 1, value_tile, 0)
        om_v[:, 0:128] = acc_v[0:ROWS, :].astype(BF16)
        om_v[:, 128:256] = acc_v[ROWS:, :].astype(BF16)

    def gate_up(b):
        @pl.when(b == 0)
        def _():
            for copy in loads[6:8]:
                copy.wait()

        for n in range(FFCOLS // 256):
            cols = pl.ds(n * 256, 256)
            gate = jnp.dot(a_v[...], wg_v[:, cols], preferred_element_type=F32)
            up = jnp.dot(a_v[...], wu_v[:, cols], preferred_element_type=F32)
            om_v[:, pl.ds(QCOLS + n * 256, 256)] = (gate * (1.0 / (1.0 + jnp.exp(-gate))) * up).astype(BF16)

    def down(half, quarter):
        cols = pl.ds(pl.multiple_of(half * 1024 + quarter * 512, 512), 512)
        return jnp.dot(om_v[...], wod_v[:, cols], preferred_element_type=F32)

    def down_other(b):
        @pl.when(b == 0)
        def _():
            for copy in loads[8:10]:
                copy.wait()
            pl.semaphore_wait(barrier, 3)

        d2d_src[b, 0] = down(1 - core, 1 - p2).astype(BF16)
        copy_of(D2D_FIRST, b).start()
        d2d_src[b, 1] = down(1 - core, p2).astype(BF16)
        copy_of(D2D_SECOND, b).start()

    def down_mine(b):
        part = down(core, 1 - p1)
        copy_of(D2D_FIRST, b).wait_recv()
        h_send[b] = (part + d2d_dst[b, 0].astype(F32)).astype(BF16)
        copy_of(RED_ONE, b).start()
        part = down(core, p1)
        copy_of(D2D_SECOND, b).wait_recv()
        h_keep[b] = part + d2d_dst[b, 1].astype(F32)

    def stage_b(b):
        copy_of(RED_ONE, b).wait_recv()
        send = pl.ds(pl.multiple_of((1 - p2) * 256, 256), 256)
        keep = pl.ds(pl.multiple_of(p2 * 256, 256), 256)
        p_send[b] = (h_keep[b, :, send] + r1_dst[b, :, send].astype(F32)).astype(BF16)
        copy_of(RED_TWO, b).start()
        p_keep[b] = h_keep[b, :, keep] + r1_dst[b, :, keep].astype(F32)

    def stage_c(b):
        copy_of(RED_TWO, b).wait_recv()
        piece = mine + p2
        x_f = x_v[rows_of(b), pl.ds(pl.multiple_of(piece * 256, 256), 256)].astype(F32)
        y_v[b, piece] = (x_f + (p_keep[b] + r2_dst[b].astype(F32))).astype(BF16)
        copy_of(GAT_ONE, b).start()
        store_y(b, piece).start()

    def stage_d(b):
        copy_of(GAT_ONE, b).wait_recv()
        copy_of(GAT_TWO, b).start()
        copy_of(OUT_FIRST, b).start()
        store_y(b, mine + 1 - p2).start()

    def stage_e(b):
        copy_of(GAT_TWO, b).wait_recv()
        copy_of(OUT_SECOND, b).start()
        store_y(b, other).start()
        store_y(b, other + 1).start()

    def stage_f(b):
        copy_of(OUT_FIRST, b).wait_recv()
        copy_of(OUT_SECOND, b).wait_recv()
        for piece in range(4):
            store_y(b, (1 - core) * 4 + piece).start()

    def when_block(b, stage):
        @pl.when((b >= 0) & (b < BLOCKS))
        def _():
            stage(b)

    def step(i, carry):
        @pl.when(i < BLOCKS)
        def _():
            project(i)
            attend(i)
            gate_up(i)
            down_other(i)

        when_block(i - LAG_B, stage_b)
        when_block(i - LAG_C, stage_c)
        when_block(i - LAG_D, stage_d)

        @pl.when(i < BLOCKS)
        def _():
            down_mine(i)

        when_block(i - LAG_E, stage_e)
        when_block(i - LAG_F, stage_f)
        return carry

    lax.fori_loop(0, BLOCKS + LAG_F, step, 0)

    def finish(b, carry):
        for kind in range(8):
            copy_of(kind, b).wait_send()
        for piece in range(8):
            store_y(b, piece).wait()
        for copy in store_kv(b):
            copy.wait()
        return carry

    lax.fori_loop(0, BLOCKS, finish, 0)


def solution(mesh):
    cos_np, sin_np = rope_tables()

    def local_layer(x_in, g_norm, w_q, w_k, w_v, w_o, w_gate, w_up, w_down):
        any_spec = pl.BlockSpec(memory_space=pl.ANY)
        y, k, v = pl.pallas_call(
            layer_kernel,
            out_shape=(jax.ShapeDtypeStruct((TOKENS, WIDTH), BF16), jax.ShapeDtypeStruct((TOKENS, HEAD_DIM), BF16),
                       jax.ShapeDtypeStruct((TOKENS, HEAD_DIM), BF16)),
            in_specs=[any_spec] * 11,
            out_specs=(any_spec,) * 3,
            scratch_shapes=[
                pltpu.VMEM((TOKENS, WIDTH), BF16),
                pltpu.VMEM((1, WIDTH), BF16),
                pltpu.VMEM((WIDTH, QCOLS + 2 * HEAD_DIM), BF16),
                pltpu.VMEM((WIDTH, FFCOLS), BF16),
                pltpu.VMEM((WIDTH, FFCOLS), BF16),
                pltpu.VMEM((KDOWN, WIDTH), BF16),
                pltpu.VMEM((TOKENS, HEAD_DIM), F32),
                pltpu.VMEM((TOKENS, HEAD_DIM), F32),
                pltpu.VMEM((ROWS, WIDTH), BF16),
                pltpu.VMEM((2 * ROWS, HEAD_DIM), BF16),
                pltpu.VMEM((TOKENS, HEAD_DIM), BF16),
                pltpu.VMEM((TOKENS, HEAD_DIM), BF16),
                pltpu.VMEM((2 * ROWS, TOKENS), F32),
                pltpu.VMEM((2 * ROWS, 128), F32),
                pltpu.VMEM((2 * ROWS, 128), F32),
                pltpu.VMEM((2 * ROWS, HEAD_DIM), F32),
                pltpu.VMEM((ROWS, KDOWN), BF16),
                pltpu.VMEM((BLOCKS, 2, ROWS, 512), BF16),
                pltpu.VMEM((BLOCKS, 2, ROWS, 512), BF16),
                pltpu.VMEM((BLOCKS, ROWS, 512), BF16),
                pltpu.VMEM((BLOCKS, ROWS, 512), F32),
                pltpu.VMEM((BLOCKS, ROWS, 512), BF16),
                pltpu.VMEM((BLOCKS, ROWS, 256), BF16),
                pltpu.VMEM((BLOCKS, ROWS, 256), F32),
                pltpu.VMEM((BLOCKS, ROWS, 256), BF16),
                pltpu.VMEM((BLOCKS, 8, ROWS, 256), BF16),
                pltpu.SemaphoreType.DMA((BLOCKS,)),
                pltpu.SemaphoreType.DMA((10,)),
                pltpu.SemaphoreType.DMA((BLOCKS, 8)),
                pltpu.SemaphoreType.DMA((2, BLOCKS)),
                pltpu.SemaphoreType.DMA((8, BLOCKS)),
                pltpu.SemaphoreType.DMA((8, BLOCKS)),
            ],
            compiler_params=pltpu.CompilerParams(collective_id=0, has_side_effects=True, vmem_limit_bytes=67043328),
        )(x_in, g_norm.reshape(1, WIDTH), w_q, w_k, w_v, w_o, w_gate, w_up, w_down, jnp.asarray(cos_np), jnp.asarray(sin_np))
        return y, k.reshape(TOKENS, 1, HEAD_DIM), v.reshape(TOKENS, 1, HEAD_DIM)

    return jax.shard_map(local_layer, mesh=mesh, in_specs=(P('dp', None), P(None), P(None, 'tp'), P(None, None), P(None, None), P('tp', None), P(None, 'tp'), P(None, 'tp'), P('tp', None)), out_specs=(P('dp', None), P('dp', 'tp', None), P('dp', 'tp', None)), check_vma=False)
```

time: 325 us -> 95.9 us (0.30)
  matrix products: 147 us -> 0 us
  waiting for transfers between devices: 95.4 us -> 0 us
  Pallas kernels: 0 us -> 85.3 us
  other arithmetic: 33.2 us -> 0 us
  local copies, waits for them, and re-layouts: 23.7 us -> 9.48 us
  between operations: 14.2 us -> 0.66 us
  loops' own time: 9.18 us -> 0 us
    dot_general x74 -> x0, matrix products: 147 us -> none  [the longest x12 60.9 us: row_block(): jnp.dot(hidden, w_down, preferred_element_type=jnp.float32)]
    psum x1 -> x0, waiting for transfers between devices: 95.3 us -> none  [local_layer(): reduced_sum = lax.psum(partial_sum, 'tp')]
    pallas_call x0 -> x1, Pallas kernels: none -> 85.3 us  [local_layer(): pl.pallas_call(layer_kernel, out_shape=(jax.ShapeDtypeStruct((TOKENS, WID...]
    dynamic_slice x24 -> x0, local copies, waits for them, and re-layouts: 18.5 us -> none  [the longest x12 10.6 us: row_block(): sin_blk = lax.dynamic_slice_in_dim(sin_tab, row_start, q_block, axis=0)]
    convert_element_type x4 -> x0, other arithmetic: 15.3 us -> none  [the longest x1 11 us: local_layer(): (x_in.astype(jnp.float32) + reduced_sum.astype(jnp.float32)).astype(jnp.b...]
    another operation x1 -> x0, loops' own time: 9.18 us -> none  [local_layer(): lax.map(row_block, jnp.arange(tokens // q_block)).reshape(tokens, width)]
    reduce_sum x13 -> x0, other arithmetic: 8.48 us -> none  [the longest x12 4.4 us: row_block(): probs_bf = jax.nn.softmax(scores, axis=-1).astype(jnp.bfloat16)]
    unnamed x12 -> x7, local copies, waits for them, and re-layouts: 1.89 us -> 8.18 us
  transfers between devices with their start and end apart: 1 -> 0, of which waited for: 1 -> 0; matrix products, arithmetic and copies ran while one was open for 0% -> 0% of each run, Pallas kernels for 0% -> 0%
where the time goes in v1:
time: 95.9 us; the launch traced here: 95.4 us
  Pallas kernels  85.3 us (89%)
  local copies, waits for them, and re-layouts  9.48 us (10%)
    pallas_call x1, Pallas kernels, local_layer(): pl.pallas_call(layer_kernel, out_shape=(jax.ShapeDtypeStruct((TOKENS, WID...  85.3 us
    unnamed x7, local copies, waits for them, and re-layouts  8.18 us

profile of v1, /device:TPU:0, one launch (start us, length us, event | category | flops | bytes accessed | tf_op | source)
XLA Modules:
  0.0 95.4 jit_solution(7748313650305053424)
XLA Ops:
  0.6 1.3 %reshape.15.g_hbm = bf16[1,2048]{1,0:T(2,128)(2,1)} reshape(bf16[2048]{0:T(1024)(128)(2,1)} %param.12) | data formatting | bytes 8192 | tf_op jit(solution)/shard_map/reshape | solution.py:351
  1.9 85.3 %shard_map.130 = (bf16[1536,2048]{1,0:T(8,128)(2,1)}, bf16[1536,128]{1,0:T(8,128)(2,1)}, bf16[1536,128]{1,0:T(8,128)(2,1)}) custom-call(bf16[1536,2048]{1,0:T(8,128)(2,1)} %x_hbm.1, bf16[1,2048]{1,0:T(2,128)(2,1)} %reshape.15.g_hbm, bf16[2048,256]{1,0:T(8,128)(2,1)} %wq_hbm.1, bf16[2048,1024]{1,0:T(8,128)(2,1)} %wk_hbm.1, bf16[2048,1024]{1,0:T(8,128)(2,1)} %wv_hbm.1, ...), custom_call_target="tpu_custom_call" | custom-call | tf_op jit(solution)/shard_map/pallas_call | solution.py:310
  87.2 0.0 copy-start.1
  87.2 0.0 copy-start
  87.2 6.7 %copy.17 = bf16[1536,2048]{1,0:T(8,128)(2,1)} copy(bf16[1536,2048]{1,0:T(8,128)(2,1)} %get-tuple-element.12) | data formatting | bytes 12582912
  93.9 0.0 copy-done.1
  93.9 0.7 copy.18
  94.6 0.0 copy-done
  94.6 0.7 copy.19
Async XLA Ops:
  87.2 6.7 %copy-start.1 = (bf16[1536,128]{1,0:T(8,128)(2,1)S(1)}, bf16[1536,128]{1,0:T(8,128)(2,1)}, u32[]{:S(2)}) copy-start(bf16[1536,128]{1,0:T(8,128)(2,1)} %get-tuple-element.7) | copy-start | bytes 1179652
  87.2 7.4 %copy-start = (bf16[1536,128]{1,0:T(8,128)(2,1)S(1)}, bf16[1536,128]{1,0:T(8,128)(2,1)}, u32[]{:S(2)}) copy-start(bf16[1536,128]{1,0:T(8,128)(2,1)} %get-tuple-element.8) | copy-start | bytes 1179652

commit v2 on v1

--- a/solution.py
+++ b/solution.py
@@ -34,11 +34,11 @@
 
 
 def layer_kernel(x_hbm, g_hbm, wq_hbm, wk_hbm, wv_hbm, wo_hbm, wg_hbm, wu_hbm, wd_hbm, cos_hbm, sin_hbm,
-                 y_out, k_out, v_out,
+                 y_v, k_v, v_v,
                  x_v, g_v, wqkv_v, wg_v, wu_v, wod_v, cos_v, sin_v,
-                 a_v, q_v, k_v, v_v, s_v, m_v, l_v, acc_v, om_v,
-                 d2d_src, d2d_dst, h_send, h_keep, r1_dst, p_send, p_keep, r2_dst, y_v,
-                 x_sem, w_sem, o_sem, kv_sem, ssem, rsem):
+                 a_v, q_v, s_v, m_v, l_v, acc_v, om_v,
+                 d2d_src, d2d_dst, h_send, h_keep, r1_dst, p_send, p_keep, r2_dst,
+                 x_sem, w_sem, ssem, rsem):
     me = lax.axis_index('tp')
     core = lax.rem(me, 2)
     xpos = lax.rem(me // 2, 2)
@@ -87,6 +87,9 @@
     mine = core * 4 + p1 * 2
     other = core * 4 + (1 - p1) * 2
 
+    def y_part(b, piece, count):
+        return y_v.at[rows_of(b), pl.ds(pl.multiple_of(piece * 256, 256), count * 256)]
+
     def copy_of(kind, b):
         if kind == D2D_FIRST or kind == D2D_SECOND:
             return remote(kind, b, d2d_src.at[b, kind], d2d_dst.at[b, kind], sibling)
@@ -95,20 +98,13 @@
         if kind == RED_TWO:
             return remote(kind, b, p_send.at[b], r2_dst.at[b], n2)
         if kind == GAT_ONE:
-            piece = mine + p2
-            return remote(kind, b, y_v.at[b, piece], y_v.at[b, piece], n2)
+            part = y_part(b, mine + p2, 1)
+            return remote(kind, b, part, part, n2)
         if kind == GAT_TWO:
-            return remote(kind, b, y_v.at[b, pl.ds(mine, 2)], y_v.at[b, pl.ds(mine, 2)], n1)
-        first = mine if kind == OUT_FIRST else other
-        return remote(kind, b, y_v.at[b, pl.ds(first, 2)], y_v.at[b, pl.ds(first, 2)], sibling)
-
-    def store_y(b, piece):
-        return pltpu.make_async_copy(y_v.at[b, piece], y_out.at[rows_of(b), pl.ds(pl.multiple_of(piece * 256, 256), 256)],
-                                     o_sem.at[b, piece])
-
-    def store_kv(b):
-        return (pltpu.make_async_copy(k_v.at[rows_of(b), :], k_out.at[rows_of(b), :], kv_sem.at[0, b]),
-                pltpu.make_async_copy(v_v.at[rows_of(b), :], v_out.at[rows_of(b), :], kv_sem.at[1, b]))
+            part = y_part(b, mine, 2)
+            return remote(kind, b, part, part, n1)
+        part = y_part(b, mine if kind == OUT_FIRST else other, 2)
+        return remote(kind, b, part, part, sibling)
 
     def project(b):
         load_x(b).wait()
@@ -122,7 +118,7 @@
             sl = pl.ds(pl.multiple_of(b * ROWS + r * 16, 16), 16)
             x_f = x_v[sl, :].astype(F32)
             inv = lax.rsqrt(jnp.mean(x_f * x_f, axis=-1, keepdims=True) + NORM_EPS)
-            a_v[pl.ds(pl.multiple_of(r * 16, 16), 16), :] = (x_f * inv * g_v[...].astype(F32)).astype(BF16)
+            a_v[pl.ds(pl.multiple_of(r * 16, 16), 16), :] = (x_f * inv * g_v[...].astype(F32)[None, :]).astype(BF16)
             return carry
 
         lax.fori_loop(0, ROWS // 16, norm_rows, 0, unroll=4)
@@ -142,8 +138,6 @@
         q_v[pl.ds(ROWS, ROWS), :] = rope(qkv[:, 128:256])
         k_v[rows_of(b), :] = rope(qkv[:, 256:384])
         v_v[rows_of(b), :] = qkv[:, 384:512].astype(BF16)
-        for copy in store_kv(b):
-            copy.start()
 
     def attend(b):
         def tile(j):
@@ -240,28 +234,23 @@
     def stage_c(b):
         copy_of(RED_TWO, b).wait_recv()
         piece = mine + p2
-        x_f = x_v[rows_of(b), pl.ds(pl.multiple_of(piece * 256, 256), 256)].astype(F32)
-        y_v[b, piece] = (x_f + (p_keep[b] + r2_dst[b].astype(F32))).astype(BF16)
+        cols = pl.ds(pl.multiple_of(piece * 256, 256), 256)
+        x_f = x_v[rows_of(b), cols].astype(F32)
+        y_v[rows_of(b), cols] = (x_f + (p_keep[b] + r2_dst[b].astype(F32))).astype(BF16)
         copy_of(GAT_ONE, b).start()
-        store_y(b, piece).start()
 
     def stage_d(b):
         copy_of(GAT_ONE, b).wait_recv()
         copy_of(GAT_TWO, b).start()
         copy_of(OUT_FIRST, b).start()
-        store_y(b, mine + 1 - p2).start()
 
     def stage_e(b):
         copy_of(GAT_TWO, b).wait_recv()
         copy_of(OUT_SECOND, b).start()
-        store_y(b, other).start()
-        store_y(b, other + 1).start()
 
     def stage_f(b):
         copy_of(OUT_FIRST, b).wait_recv()
         copy_of(OUT_SECOND, b).wait_recv()
-        for piece in range(4):
-            store_y(b, (1 - core) * 4 + piece).start()
 
     def when_block(b, stage):
         @pl.when((b >= 0) & (b < BLOCKS))
@@ -293,10 +282,6 @@
     def finish(b, carry):
         for kind in range(8):
             copy_of(kind, b).wait_send()
-        for piece in range(8):
-            store_y(b, piece).wait()
-        for copy in store_kv(b):
-            copy.wait()
         return carry
 
     lax.fori_loop(0, BLOCKS, finish, 0)
@@ -309,13 +294,12 @@
         any_spec = pl.BlockSpec(memory_space=pl.ANY)
         y, k, v = pl.pallas_call(
             layer_kernel,
-            out_shape=(jax.ShapeDtypeStruct((TOKENS, WIDTH), BF16), jax.ShapeDtypeStruct((TOKENS, HEAD_DIM), BF16),
-                       jax.ShapeDtypeStruct((TOKENS, HEAD_DIM), BF16)),
+            out_shape=(pltpu.VMEM((TOKENS, WIDTH), BF16), pltpu.VMEM((TOKENS, HEAD_DIM), BF16), pltpu.VMEM((TOKENS, HEAD_DIM), BF16)),
             in_specs=[any_spec] * 11,
-            out_specs=(any_spec,) * 3,
+            out_specs=(pl.BlockSpec(memory_space=pltpu.VMEM),) * 3,
             scratch_shapes=[
                 pltpu.VMEM((TOKENS, WIDTH), BF16),
-                pltpu.VMEM((1, WIDTH), BF16),
+                pltpu.VMEM((WIDTH,), BF16),
                 pltpu.VMEM((WIDTH, QCOLS + 2 * HEAD_DIM), BF16),
                 pltpu.VMEM((WIDTH, FFCOLS), BF16),
                 pltpu.VMEM((WIDTH, FFCOLS), BF16),
@@ -324,8 +308,6 @@
                 pltpu.VMEM((TOKENS, HEAD_DIM), F32),
                 pltpu.VMEM((ROWS, WIDTH), BF16),
                 pltpu.VMEM((2 * ROWS, HEAD_DIM), BF16),
-                pltpu.VMEM((TOKENS, HEAD_DIM), BF16),
-                pltpu.VMEM((TOKENS, HEAD_DIM), BF16),
                 pltpu.VMEM((2 * ROWS, TOKENS), F32),
                 pltpu.VMEM((2 * ROWS, 128), F32),
                 pltpu.VMEM((2 * ROWS, 128), F32),
@@ -339,16 +321,13 @@
                 pltpu.VMEM((BLOCKS, ROWS, 256), BF16),
                 pltpu.VMEM((BLOCKS, ROWS, 256), F32),
                 pltpu.VMEM((BLOCKS, ROWS, 256), BF16),
-                pltpu.VMEM((BLOCKS, 8, ROWS, 256), BF16),
                 pltpu.SemaphoreType.DMA((BLOCKS,)),
                 pltpu.SemaphoreType.DMA((10,)),
-                pltpu.SemaphoreType.DMA((BLOCKS, 8)),
-                pltpu.SemaphoreType.DMA((2, BLOCKS)),
                 pltpu.SemaphoreType.DMA((8, BLOCKS)),
                 pltpu.SemaphoreType.DMA((8, BLOCKS)),
             ],
-            compiler_params=pltpu.CompilerParams(collective_id=0, has_side_effects=True, vmem_limit_bytes=67043328),
-        )(x_in, g_norm.reshape(1, WIDTH), w_q, w_k, w_v, w_o, w_gate, w_up, w_down, jnp.asarray(cos_np), jnp.asarray(sin_np))
+            compiler_params=pltpu.CompilerParams(collective_id=0, has_side_effects=True, vmem_limit_bytes=67043328 - 8 * 1024 * 1024),
+        )(x_in, g_norm, w_q, w_k, w_v, w_o, w_gate, w_up, w_down, jnp.asarray(cos_np), jnp.asarray(sin_np))
         return y, k.reshape(TOKENS, 1, HEAD_DIM), v.reshape(TOKENS, 1, HEAD_DIM)
 
     return jax.shard_map(local_layer, mesh=mesh, in_specs=(P('dp', None), P(None), P(None, 'tp'), P(None, None), P(None, None), P('tp', None), P(None, 'tp'), P(None, 'tp'), P('tp', None)), out_specs=(P('dp', None), P('dp', 'tp', None), P('dp', 'tp', None)), check_vma=False)

time: 95.9 us -> 89.6 us (0.934)
  local copies, waits for them, and re-layouts: 9.48 us -> 4.2 us
    unnamed x7 -> x3, local copies, waits for them, and re-layouts: 8.18 us -> 4.2 us
    reshape x1 -> x0, local copies, waits for them, and re-layouts: 1.29 us -> none  [local_layer(): g_norm.reshape(1, WIDTH)]
where the time goes in v2:
time: 89.6 us; the launch traced here: 89.5 us
  Pallas kernels  84.6 us (94%)
  local copies, waits for them, and re-layouts  4.2 us (5%)
    pallas_call x1, Pallas kernels, local_layer(): pl.pallas_call(layer_kernel, out_shape=(pltpu.VMEM((TOKENS, WIDTH), BF16)...  84.6 us
    unnamed x3, local copies, waits for them, and re-layouts  4.2 us

profile of v2, /device:TPU:0, one launch (start us, length us, event | category | flops | bytes accessed | tf_op | source)
XLA Modules:
  0.0 89.5 jit_solution(16121206252285195846)
XLA Ops:
  0.6 84.6 %shard_map.130 = (bf16[1536,2048]{1,0:T(8,128)(2,1)S(1)}, bf16[1536,128]{1,0:T(8,128)(2,1)S(1)}, bf16[1536,128]{1,0:T(8,128)(2,1)S(1)}) custom-call(bf16[1536,2048]{1,0:T(8,128)(2,1)} %x_hbm.1, bf16[2048]{0:T(1024)(128)(2,1)} %g_hbm.1, bf16[2048,256]{1,0:T(8,128)(2,1)} %wq_hbm.1, bf16[2048,1024]{1,0:T(8,128)(2,1)} %wk_hbm.1, bf16[2048,1024]{1,0:T(8,128)(2,1)} %wv_hbm.1, ...), custom_call_target="tpu_custom_call" | custom-call | tf_op jit(solution)/shard_map/pallas_call | solution.py:295
  85.3 2.7 %copy.17 = bf16[1536,2048]{1,0:T(8,128)(2,1)} copy(bf16[1536,2048]{1,0:T(8,128)(2,1)S(1)} %get-tuple-element.9) | data formatting | bytes 12582912
  88.0 0.7 copy.18
  88.7 0.7 copy.19
